TPU v7x, 512 devices: a 8x2x16 block of a 8x16x16 slice. The times are simulated.
512 devices in a mesh: groups: 2 (over y), seq: 32 (over z, core), rep: 8 (over x).
Axes of the slice: x: 8, y: 2, z: 16, core: 2. Of those that a mesh axis runs over, the one named last changes fastest.
The devices are a block of a 8x16x16 slice.
Arguments:
- queries: bfloat16 [1024, 4096], P(('groups', 'seq'), 'rep'), parts along dimension 0, may hold values from -128 to 128
- keys_new: bfloat16 [1024, 1024], P(('groups', 'seq'), 'rep'), parts along dimension 0, may hold values from -4 to 4
- values_new: bfloat16 [1024, 1024], P(('groups', 'seq'), 'rep'), parts along dimension 0, may hold values from -6 to 6
- keys_past: bfloat16 [16384, 1024], P(('groups', 'seq'), 'rep'), parts along dimension 0, may hold values from -4 to 4
- values_past: bfloat16 [16384, 1024], P(('groups', 'seq'), 'rep'), parts along dimension 0, may hold values from -6 to 6
- block_order: int32 [64], P('groups'), parts along dimension 0, may hold values from 0 to 31, each once
- residual: bfloat16 [1024, 4096], P(('groups', 'seq'), 'rep'), parts along dimension 0, may hold values from -6 to 6
- out_proj: bfloat16 [4096, 4096], P('seq', 'rep'), may hold values from -0.09375 to 0.09375
- norm_gain: float32 [4096], replicated, may hold values from 0.5 to 1.5
- router: float32 [4096, 4], replicated, may hold values from -0.09375 to 0.09375
- w_gate: bfloat16 [8, 4096, 4096], P('rep', None, 'seq'), may hold values from -0.09375 to 0.09375
- w_up: bfloat16 [8, 4096, 4096], P('rep', None, 'seq'), may hold values from -0.09375 to 0.09375
- w_down: bfloat16 [8, 4096, 4096], P('rep', 'seq'), may hold values from -0.0625 to 0.0625
- expert_ids: int32 [1024, 2], P(('groups', 'seq')), parts along dimension 0, may hold values from 0 to 3, all different within a row; in each aligned block of 16 rows (0 to 15, 16 to 31, ...) at most 12 rows name the same one
Outputs:
- attended: bfloat16 [1024, 4096], P(('groups', 'seq'), 'rep'), parts along dimension 0
- layer_out: bfloat16 [1024, 4096], P(('groups', 'seq'), 'rep'), parts along dimension 0
- keys_cache: bfloat16 [1024, 1024], P(('groups', 'seq')), parts along dimension 0
- values_cache: bfloat16 [1024, 1024], P(('groups', 'seq')), parts along dimension 0
There are 2 independent parts, one for each index of `groups`. A program takes and returns all parts, laid end to end along the dimension named above; an argument that names none is the same for every part. Nothing has to cross between parts.
Inputs may be any that keep to these rules, and one draw needn't show every extreme that they name: `block_order`: each block index 0 to 32 - 1 appears once. `expert_ids`: each row names 2 different experts; in the rows of one device (aligned blocks of 16 rows) no expert is named by more than 12 rows, and in some block one expert is named by exactly 12.
All inputs are finite; a program needn't handle non-finite values.
Results may differ from a plain program's by a relative error of at most 0.011.
Values may be sent and summed in bfloat16 or wider, within the bound.
A program may use at most 64 MiB of HBM per device.

v0:
```python
import math
import jax
import jax.numpy as jnp
from jax import lax
from jax.sharding import Mesh
from jax.sharding import PartitionSpec as P

EXPERTS = 4
CAP = 12
SEQ = ("seq_0", "seq_1")
GROUPS_SEQ = ("groups", "seq_0", "seq_1")


def in_one_piece(arrays, axis, dim, along):
    both = jnp.concatenate(arrays, axis=along)
    out, at, gathered = (lax.all_gather(both, axis, axis=dim, tiled=True), 0, [])
    for a in arrays:
        gathered.append(lax.slice_in_dim(out, at, at + a.shape[along], axis=along))
        at += a.shape[along]
    return tuple(gathered)


def sent_to_all(array, axis):
    size = lax.axis_size(axis)
    return lax.all_to_all(
        jnp.broadcast_to(array[None], (size, *array.shape)), axis, 0, 0, tiled=True
    )


def laid_out(tiles, dim):
    tiles = jnp.moveaxis(tiles, 0, dim)
    shape = tiles.shape
    return tiles.reshape(*shape[:dim], shape[dim] * shape[dim + 1], *shape[dim + 2 :])


def gather_directly(array, axis, dim):
    tiles = sent_to_all(array, axis)
    return laid_out(tiles, dim)


def own_block(tiles, axes, order):
    shape = [lax.axis_size(a) for a in axes]
    tiles = tiles.reshape(*shape, *tiles.shape[1:])
    tiles = tiles.transpose(*order, *range(len(axes), tiles.ndim))
    tiles = tiles.reshape(-1, *tiles.shape[len(axes) :])
    for k in order:
        tiles = lax.psum_scatter(tiles, axes[k], scatter_dimension=0, tiled=True)
    return tiles[0]


def in_blocks(array, dim, size):
    shape = array.shape
    tiles = array.reshape(*shape[:dim], size, shape[dim] // size, *shape[dim + 1 :])
    return jnp.moveaxis(tiles, dim, 0)


def sum_by_axis(array, axes, order, dim):
    size = lax.axis_size(axes)
    return own_block(in_blocks(array, dim, size), axes, order)


def block_lookup(owners, block_order):
    width = block_order.shape[0]
    hits = owners[:, None] == jnp.arange(width, dtype=jnp.int32)[None, :]
    return jnp.sum(jnp.where(hits, block_order[None, :], 0), axis=1)


def body(
    queries,
    keys_new,
    values_new,
    keys_past,
    values_past,
    block_order,
    residual,
    out_proj,
    norm_gain,
    router,
    w_gate,
    w_up,
    w_down,
    expert_ids,
):
    seq_index = lax.axis_index(SEQ)
    rep_index = lax.axis_index("rep")
    rep_count = lax.axis_size("rep")
    tok_count = queries.shape[0]
    head_dim = keys_new.shape[1]
    q_per = queries.shape[1] // head_dim
    past_len = keys_past.shape[0]
    key_span = past_len + tok_count
    row_total = tok_count * q_per
    my_block = block_lookup(jnp.full((1,), seq_index, jnp.int32), block_order)[0]
    scaling = 1.0 / math.sqrt(head_dim)
    query_rows = queries.reshape(row_total, head_dim)
    query_pos = my_block * tok_count + jnp.arange(row_total, dtype=jnp.int32) // q_per
    keys_local = jnp.concatenate([keys_past, keys_new], axis=0)
    values_local = jnp.concatenate([values_past, values_new], axis=0)
    running = jnp.full((row_total,), -1e30, jnp.float32)
    key_piece, value_piece = in_one_piece((keys_local, values_local), SEQ, 0, 1)
    row_count = key_piece.shape[0]
    key_index = jnp.arange(row_count, dtype=jnp.int32)
    key_owner = key_index // key_span
    offset = key_index % key_span
    key_pos = block_lookup(key_owner, block_order) * tok_count + offset - past_len
    visible = (offset < past_len)[None, :] | (key_pos[None, :] <= query_pos[:, None])
    scores = jnp.dot(query_rows, key_piece.T, preferred_element_type=jnp.float32) * scaling
    highest = jnp.maximum(running, jnp.max(jnp.where(visible, scores, -1e30), axis=1))
    weights = jnp.where(visible, jnp.exp(scores - highest[:, None]), 0.0)
    totals = jnp.sum(weights, axis=1)
    numerator = jnp.dot(
        weights.astype(jnp.bfloat16), value_piece, preferred_element_type=jnp.float32
    )
    running, totals, numerator = (highest, totals, numerator)
    attn_local = (
        (numerator / totals[:, None]).reshape(tok_count, q_per * head_dim).astype(jnp.bfloat16)
    )
    attn_full, keys_cache, values_cache = (
        lax.all_gather(attn_local, "rep", axis=1, tiled=True),
        *in_one_piece((keys_new, values_new), "rep", 1, 0),
    )
    projected = jnp.dot(
        attn_full,
        lax.all_gather(out_proj, SEQ, axis=0, tiled=True),
        preferred_element_type=jnp.float32,
    )
    attended = (residual.astype(jnp.float32) + projected).astype(jnp.bfloat16)
    full_rows = gather_directly(attended, "rep", 1)
    features = full_rows.astype(jnp.float32)
    mean_square = jnp.mean(features * features, axis=1, keepdims=True)
    normed = (features * norm_gain[None, :] * lax.rsqrt(mean_square + 1e-05)).astype(jnp.bfloat16)
    logits = jnp.dot(normed.astype(jnp.float32), router, precision=lax.Precision.HIGHEST)
    expert_range = jnp.arange(EXPERTS, dtype=jnp.int32)
    first_pick = (expert_ids[:, 0:1] == expert_range[None, :]).astype(jnp.float32)
    second_pick = (expert_ids[:, 1:2] == expert_range[None, :]).astype(jnp.float32)
    share_first = jax.nn.sigmoid(
        jnp.sum(first_pick * logits, axis=1) - jnp.sum(second_pick * logits, axis=1)
    )
    token_share = share_first[:, None] * first_pick + (1.0 - share_first)[:, None] * second_pick
    member = first_pick + second_pick
    ranking = jnp.cumsum(member, axis=0) - member
    slot_range = jnp.arange(CAP, dtype=jnp.float32)
    selection = member.T[:, None, :] * (ranking.T[:, None, :] == slot_range[None, :, None]).astype(
        jnp.float32
    )
    mine_mask = (expert_range == rep_index % EXPERTS).astype(jnp.float32)
    my_selection = jnp.einsum("e,ejt->jt", mine_mask, selection)
    slot_rows = jnp.dot(
        my_selection.astype(jnp.bfloat16), normed, preferred_element_type=jnp.float32
    ).astype(jnp.bfloat16)
    gate_local = w_gate[0]
    up_local = w_up[0]
    down_local = w_down[0]
    piece = lax.all_gather(slot_rows, SEQ, axis=0, tiled=True)
    gate_part = jnp.dot(piece, gate_local, preferred_element_type=jnp.float32)
    up_part = jnp.dot(piece, up_local, preferred_element_type=jnp.float32)
    hidden_slots = (jax.nn.silu(gate_part) * up_part).astype(jnp.bfloat16)
    expert_part = sum_by_axis(
        jnp.dot(hidden_slots, down_local, preferred_element_type=jnp.float32).astype(jnp.bfloat16),
        SEQ,
        (1, 0),
        0,
    ).astype(jnp.float32)
    returned = lax.all_to_all(
        expert_part.astype(jnp.bfloat16), "rep", split_axis=1, concat_axis=0, tiled=True
    ).astype(expert_part.dtype)
    source_expert = jnp.arange(rep_count, dtype=jnp.int32) % EXPERTS
    source_pick = (source_expert[:, None] == expert_range[None, :]).astype(jnp.float32)
    combine = jnp.einsum("re,ejt,te->trj", source_pick, selection, token_share).reshape(
        tok_count, rep_count * CAP
    )
    moe_slice = jnp.dot(combine, returned, precision=lax.Precision.HIGHEST)
    layer_out = (attended.astype(jnp.float32) + moe_slice).astype(jnp.bfloat16)
    return (attended, layer_out, keys_cache, values_cache)


def solution(mesh):
    split = Mesh(
        mesh.devices.reshape(mesh.shape["groups"], 16, 2, mesh.shape["rep"]),
        ("groups", "seq_0", "seq_1", "rep"),
    )
    return jax.shard_map(
        body,
        mesh=split,
        in_specs=(
            P(GROUPS_SEQ, "rep"),
            P(GROUPS_SEQ, "rep"),
            P(GROUPS_SEQ, "rep"),
            P(GROUPS_SEQ, "rep"),
            P(GROUPS_SEQ, "rep"),
            P("groups"),
            P(GROUPS_SEQ, "rep"),
            P(SEQ, "rep"),
            P(),
            P(),
            P("rep", None, SEQ),
            P("rep", None, SEQ),
            P("rep", SEQ, None),
            P(GROUPS_SEQ, None),
        ),
        out_specs=(
            P(GROUPS_SEQ, "rep"),
            P(GROUPS_SEQ, "rep"),
            P(GROUPS_SEQ, None),
            P(GROUPS_SEQ, None),
        ),
        check_vma=False,
    )
```

profile of v0, /device:TPU:66, one launch (start us, length us, event | category | flops | bytes accessed | tf_op | source)
XLA Modules:
  0.0 435.2 jit_solution(9324647808169427397)
XLA Ops:
  7.3 1.7 maximum_maximum_fusion
  9.0 0.7 all-gather.7.cloned.1.call-update
  9.8 0.7 reshape.156
  10.5 1.3 fusion.64
  12.5 0.9 select_reduce_fusion.1
  13.5 106.4 %all-gather.5.cloned.1.call-done = bf16[8704,256]{1,0:T(8,128)(2,1)} async-done(((bf16[272,256]{1,0:T(8,128)(2,1)}), bf16[8704,256]{1,0:T(8,128)(2,1)}) %all-gather.5.cloned.1.call-update) | async-done | bytes 4456464 | tf_op jit(solution)/shard_map/all_gather | solution.py:16
  119.9 2.8 select_reduce_fusion
  122.7 0.9 fusion.5
  123.6 0.8 fusion.22
  124.5 24.7 %all_gather.16 = bf16[16,4096]{1,0:T(8,128)(2,1)S(1)} all-gather(bf16[16,512]{1,0:T(8,128)(2,1)S(1)} %convert_element_type.81), channel_id=1, replica_groups=mesh['groups'=2,'seq_0'=16,'seq_1'=2,'rep'=8] {'rep'}, dimensions={1}, use_global_device_ids=true | all-gather | bytes 147456 | tf_op jit(solution)/shard_map/all_gather | solution.py:119
  149.2 44.8 %all-gather.7.cloned.1.call-done = bf16[4096,512]{1,0:T(8,128)(2,1)} async-done(((bf16[128,512]{1,0:T(8,128)(2,1)}), bf16[4096,512]{1,0:T(8,128)(2,1)}) %all-gather.7.cloned.1.call-update) | async-done | bytes 4194320 | tf_op jit(solution)/shard_map/all_gather | solution.py:124
  194.0 2.8 fusion.16
  196.8 0.7 broadcast_in_dim.33
  197.5 7.2 %all-to-all-start = ((bf16[8,16,512]{2,1,0:T(8,128)(2,1)}), bf16[8,16,512]{2,1,0:T(8,128)(2,1)S(1)}, u32[]{:S(2)}, u32[]{:S(2)}) async-start(bf16[8,16,512]{2,1,0:T(8,128)(2,1)} %broadcast_in_dim.33), calls=%async_computation | async-start | bytes 262144 | tf_op jit(solution)/shard_map/all_to_all | solution.py:25
  204.8 8.0 %all-to-all-done = bf16[8,16,512]{2,1,0:T(8,128)(2,1)S(1)} async-done(((bf16[8,16,512]{2,1,0:T(8,128)(2,1)}), bf16[8,16,512]{2,1,0:T(8,128)(2,1)S(1)}, u32[]{:S(2)}, u32[]{:S(2)}) %all-to-all-start) | async-done | bytes 131104 | tf_op jit(solution)/shard_map/all_to_all | solution.py:25
  213.7 0.9 fusion.1
  214.7 68.2 %all-gather.9.cloned.1.call-done = bf16[32,12,4096]{2,1,0:T(8,128)(2,1)} async-done(((bf16[1,12,4096]{2,1,0:T(8,128)(2,1)}), bf16[32,12,4096]{2,1,0:T(8,128)(2,1)}) %all-gather.9.cloned.1.call-update) | async-done | bytes 3145744 | tf_op jit(solution)/shard_map/all_gather | solution.py:154
  282.9 5.6 %reshape.160 = bf16[384,4096]{1,0:T(8,128)(2,1)} reshape(bf16[32,12,4096]{2,1,0:T(8,128)(2,1)} %all-gather.9.cloned.1.call-done) | data formatting | bytes 6291456
  288.5 2.9 fusion.30
  291.5 7.0 %convolution_convert_fusion = bf16[384,4096]{1,0:T(8,128)(2,1)} fusion(bf16[384,4096]{1,0:T(8,128)(2,1)} %reshape.160, bf16[1,128,4096]{2,1,0:T(8,128)(2,1)S(1)} %copy-done, bf16[1,4096,128]{2,1,0:T(8,128)(2,1)S(1)} %copy-done.2, f32[384,128]{1,0:T(8,128)S(1)} %fusion.30), kind=kOutput, calls=%fused_computation.2 | convolution fusion | flops 807174144 | bytes 8585216 | tf_op jit(solution)/shard_map/dot_general | solution.py:159
  298.5 5.5 %reshape_reshape.3 = bf16[16,2,12,4096]{3,2,1,0:T(8,128)(2,1)} reshape(bf16[384,4096]{1,0:T(8,128)(2,1)} %convolution_convert_fusion) | data formatting | bytes 6291456 | tf_op jit(solution)/shard_map/reshape;reshape | solution.py:43
  304.0 5.6 %copy.51 = bf16[2,16,12,4096]{3,1,0,2:T(8,128)(2,1)} copy(bf16[2,16,12,4096]{3,2,0,1:T(8,128)(2,1)} %bitcast.62) | data formatting | bytes 6291456 | tf_op jit(solution)/shard_map/transpose | solution.py:44
  309.9 19.5 %reduce-scatter.3.cloned.1.call-done = bf16[16,12,4096]{2,0,1:T(8,128)(2,1)} async-done(((bf16[32,12,4096]{2,0,1:T(8,128)(2,1)}), bf16[16,12,4096]{2,0,1:T(8,128)(2,1)}) %reduce-scatter.3.cloned.1.call-update) | async-done | bytes 1572880 | tf_op jit(solution)/shard_map/reduce_scatter | solution.py:47
  329.5 3.7 copy.52
  333.2 22.3 %all_gather.19 = bf16[32,1024]{1,0:T(8,128)(2,1)S(1)} all-gather(bf16[32,128]{1,0:T(8,128)(2,1)S(1)} %pad_maximum_fusion), channel_id=1, replica_groups=mesh['groups'=2,'seq_0'=16,'seq_1'=2,'rep'=8] {'rep'}, dimensions={1}, use_global_device_ids=true | all-gather | bytes 73728 | tf_op jit(solution)/shard_map/all_gather | solution.py:16
  355.6 0.6 fusion.72
  356.2 54.9 %reduce-scatter.5.cloned.1.call-done = bf16[1,12,4096]{2,1,0:T(8,128)(2,1)} async-done(((bf16[16,12,4096]{2,1,0:T(8,128)(2,1)}), bf16[1,12,4096]{2,1,0:T(8,128)(2,1)}) %reduce-scatter.5.cloned.1.call-update) | async-done | bytes 98320 | tf_op jit(solution)/shard_map/reduce_scatter | solution.py:47
  411.1 0.9 copy.57
  412.0 0.7 copy.53
  412.7 7.4 %all-to-all-start.1 = ((bf16[12,8,512]{2,0,1:T(8,128)(2,1)}), bf16[12,8,512]{2,0,1:T(8,128)(2,1)S(1)}, u32[]{:S(2)}, u32[]{:S(2)}) async-start(bf16[12,8,512]{2,0,1:T(8,128)(2,1)} %copy.53), calls=%async_computation.3 | async-start | bytes 262144 | tf_op jit(solution)/shard_map/all_to_all | solution.py:164
  420.4 7.4 %all-to-all-done.1 = bf16[12,8,512]{2,0,1:T(8,128)(2,1)S(1)} async-done(((bf16[12,8,512]{2,0,1:T(8,128)(2,1)}), bf16[12,8,512]{2,0,1:T(8,128)(2,1)S(1)}, u32[]{:S(2)}, u32[]{:S(2)}) %all-to-all-start.1) | async-done | bytes 98336 | tf_op jit(solution)/shard_map/all_to_all | solution.py:164
  427.8 0.8 fusion.15
  (54 shorter events, 1.9 us)
Async XLA Ops:
  7.2 284.3 %copy-start = (bf16[1,128,4096]{2,1,0:T(8,128)(2,1)S(1)}, bf16[1,128,4096]{2,1,0:T(8,128)(2,1)}, u32[]{:S(2)}) copy-start(bf16[1,128,4096]{2,1,0:T(8,128)(2,1)} %param.26) | copy-start | bytes 3145732
  7.2 112.7 %all-gather.5.cloned.1.call-start = ((), (), s32[]{:S(2)}) async-start(), calls=%async_computation.4 | async-start | bytes 4595712 | tf_op jit(solution)/shard_map/all_gather | solution.py:16
  9.0 185.0 %all-gather.7.cloned.1.call-start = ((), (), s32[]{:S(2)}) async-start(), calls=%async_computation.5 | async-start | bytes 4325376 | tf_op jit(solution)/shard_map/all_gather | solution.py:124
  119.9 3.7 copy-start.10
  123.6 70.4 %copy-start.6 = (bf16[16,512]{1,0:T(8,128)(2,1)S(1)}, bf16[16,512]{1,0:T(8,128)(2,1)}, u32[]{:S(2)}) copy-start(bf16[16,512]{1,0:T(8,128)(2,1)} %param.20) | copy-start | bytes 49156
  149.2 55.5 %copy-start.9 = (s32[16,2]{0,1:T(2,128)S(1)}, s32[16,2]{0,1:T(2,128)}, u32[]{:S(2)}) copy-start(s32[16,2]{0,1:T(2,128)} %param.27) | copy-start | bytes 388
  149.2 63.7 %copy-start.4 = (f32[4096,4]{0,1:T(4,128)S(1)}, f32[4096,4]{0,1:T(4,128)}, u32[]{:S(2)}) copy-start(f32[4096,4]{0,1:T(4,128)} %param.23) | copy-start | bytes 196612
  149.2 63.8 %copy-start.5 = (f32[4096]{0:T(1024)S(1)}, f32[4096]{0:T(1024)}, u32[]{:S(2)}) copy-start(f32[4096]{0:T(1024)} %param.22) | copy-start | bytes 49156
  196.8 231.0 %copy-start.3 = (bf16[16,512]{1,0:T(8,128)(2,1)}, bf16[16,512]{1,0:T(8,128)(2,1)S(1)}, u32[]{:S(2)}) copy-start(bf16[16,512]{1,0:T(8,128)(2,1)S(1)} %fusion.16) | copy-start | bytes 49156
  197.5 15.2 %all-to-all-start = ((bf16[8,16,512]{2,1,0:T(8,128)(2,1)}), bf16[8,16,512]{2,1,0:T(8,128)(2,1)S(1)}, u32[]{:S(2)}, u32[]{:S(2)}) async-start(bf16[8,16,512]{2,1,0:T(8,128)(2,1)} %broadcast_in_dim.33), calls=%async_computation | async-start | bytes 262144 | tf_op jit(solution)/shard_map/all_to_all | solution.py:25
  204.7 78.2 %all-gather.9.cloned.1.call-start = ((), (), s32[]{:S(2)}) async-start(), calls=%async_computation.8 | async-start | bytes 4325376 | tf_op jit(solution)/shard_map/all_gather | solution.py:154
  214.6 73.9 %copy-start.1 = (bf16[1,4096,128]{2,1,0:T(8,128)(2,1)S(1)}, bf16[1,4096,128]{2,1,0:T(8,128)(2,1)}, u32[]{:S(2)}) copy-start(bf16[1,4096,128]{2,1,0:T(8,128)(2,1)} %param.24) | copy-start | bytes 3145732
  214.6 114.8 %reduce-scatter.3.cloned.1.call-start = ((), (), s32[]{:S(2)}) async-start(), calls=%async_computation.6 | async-start | bytes 4718592 | tf_op jit(solution)/shard_map/reduce_scatter | solution.py:47
  288.5 3.0 copy-start.2
  309.7 23.5 %copy-start.7 = (bf16[16,128]{1,0:T(8,128)(2,1)S(1)}, bf16[16,128]{1,0:T(8,128)(2,1)}, u32[]{:S(2)}) copy-start(bf16[16,128]{1,0:T(8,128)(2,1)} %param.16) | copy-start | bytes 12292
  309.7 23.5 %copy-start.8 = (bf16[16,128]{1,0:T(8,128)(2,1)S(1)}, bf16[16,128]{1,0:T(8,128)(2,1)}, u32[]{:S(2)}) copy-start(bf16[16,128]{1,0:T(8,128)(2,1)} %param.15) | copy-start | bytes 12292
  309.7 101.4 %reduce-scatter.5.cloned.1.call-start = ((), (), s32[]{:S(2)}) async-start(), calls=%async_computation.7 | async-start | bytes 2228224 | tf_op jit(solution)/shard_map/reduce_scatter | solution.py:47
  412.7 15.1 %all-to-all-start.1 = ((bf16[12,8,512]{2,0,1:T(8,128)(2,1)}), bf16[12,8,512]{2,0,1:T(8,128)(2,1)S(1)}, u32[]{:S(2)}, u32[]{:S(2)}) async-start(bf16[12,8,512]{2,0,1:T(8,128)(2,1)} %copy.53), calls=%async_computation.3 | async-start | bytes 262144 | tf_op jit(solution)/shard_map/all_to_all | solution.py:164
Sparse Core Ops, SparseCore 0:
  10.2 109.7 all-gather.4
  122.1 71.8 all-gather.6
  214.7 68.1 all-gather.8
  309.8 19.6 reduce-scatter.2
  333.3 77.7 reduce-scatter.4
where the time goes:
time: 436 us; the launch traced here: 435 us
  waiting for transfers between devices  310 us (71%)
  blocking collectives  47 us (11%)
  local copies, waits for them, and re-layouts  24.3 us (6%)
  matrix products  18.8 us (4%)
  starting transfers between devices  15.1 us (3%)
  between operations  14.7 us (3%)
  other arithmetic  5.04 us (1%)
    all_gather x1, waiting for transfers between devices, in_one_piece(): lax.all_gather(both, axis, axis=dim, tiled=True)  106 us
    reduce_scatter x2, waiting for transfers between devices, own_block(): tiles = lax.psum_scatter(tiles, axes[k], scatter_dimension=0, tiled=True)  74.4 us
    all_gather x1, waiting for transfers between devices, body(): piece = lax.all_gather(slot_rows, SEQ, axis=0, tiled=True)  68.2 us
    all_gather x1, waiting for transfers between devices, body(): lax.all_gather(out_proj, SEQ, axis=0, tiled=True)  44.8 us
    all_gather x1, blocking collectives, body(): lax.all_gather(attn_local, 'rep', axis=1, tiled=True)  24.7 us
    all_gather x1, blocking collectives, in_one_piece(): lax.all_gather(both, axis, axis=dim, tiled=True)  22.3 us
  transfers between devices with their start and end apart: 7, of which 7 were waited for; matrix products, arithmetic and copies ran while one was open for 2% of the time, Pallas kernels for 0%

commit v1 on v0

--- a/solution.py
+++ b/solution.py
@@ -9,6 +9,11 @@
 CAP = 12
 SEQ = ("seq_0", "seq_1")
 GROUPS_SEQ = ("groups", "seq_0", "seq_1")
+
+
+def gather_from_all(x, axis, dim):
+    copies = jnp.concatenate([x] * lax.axis_size(axis), axis=dim)
+    return lax.all_to_all(copies, axis, dim, dim, tiled=True)
 
 
 def in_one_piece(arrays, axis, dim, along):
@@ -116,7 +121,7 @@
         (numerator / totals[:, None]).reshape(tok_count, q_per * head_dim).astype(jnp.bfloat16)
     )
     attn_full, keys_cache, values_cache = (
-        lax.all_gather(attn_local, "rep", axis=1, tiled=True),
+        gather_from_all(attn_local, "rep", 1),
         *in_one_piece((keys_new, values_new), "rep", 1, 0),
     )
     projected = jnp.dot(

time: 436 us -> 436 us (level)
  waiting for transfers between devices: 310 us -> 320 us
  blocking collectives: 47 us -> 37.4 us
    all_gather x1 -> x0, blocking collectives: 24.7 us -> none  [body(): lax.all_gather(attn_local, 'rep', axis=1, tiled=True)]
    all_to_all x0 -> x1, blocking collectives: none -> 15 us  [gather_from_all(): return lax.all_to_all(copies, axis, dim, dim, tiled=True)]
    all_gather x1, waiting for transfers between devices: 44.8 us -> 54.4 us  [body(): lax.all_gather(out_proj, SEQ, axis=0, tiled=True)]
where the time goes in v1:
time: 436 us; the launch traced here: 435 us
  waiting for transfers between devices  320 us (73%)
  blocking collectives  37.4 us (9%)
  local copies, waits for them, and re-layouts  24.3 us (6%)
  matrix products  18.8 us (4%)
  starting transfers between devices  14.8 us (3%)
  between operations  14.7 us (3%)
  other arithmetic  5.04 us (1%)
    all_gather x1, waiting for transfers between devices, in_one_piece(): lax.all_gather(both, axis, axis=dim, tiled=True)  106 us
    reduce_scatter x2, waiting for transfers between devices, own_block(): tiles = lax.psum_scatter(tiles, axes[k], scatter_dimension=0, tiled=True)  74.7 us
    all_gather x1, waiting for transfers between devices, body(): piece = lax.all_gather(slot_rows, SEQ, axis=0, tiled=True)  68.2 us
    all_gather x1, waiting for transfers between devices, body(): lax.all_gather(out_proj, SEQ, axis=0, tiled=True)  54.4 us
    all_gather x1, blocking collectives, in_one_piece(): lax.all_gather(both, axis, axis=dim, tiled=True)  22.4 us
    all_to_all x1, blocking collectives, gather_from_all(): return lax.all_to_all(copies, axis, dim, dim, tiled=True)  15 us
  transfers between devices with their start and end apart: 7, of which 7 were waited for; matrix products, arithmetic and copies ran while one was open for 2% of the time, Pallas kernels for 0%

profile of v1, /device:TPU:66, one launch (start us, length us, event | category | flops | bytes accessed | tf_op | source)
XLA Modules:
  0.0 435.2 jit_solution(3757974615029496302)
XLA Ops:
  7.3 1.7 maximum_maximum_fusion
  9.0 0.7 all-gather.7.cloned.1.call-update
  9.8 0.7 reshape.179
  10.5 1.3 fusion.64
  12.5 0.9 select_reduce_fusion.1
  13.5 106.4 %all-gather.5.cloned.1.call-done = bf16[8704,256]{1,0:T(8,128)(2,1)} async-done(((bf16[272,256]{1,0:T(8,128)(2,1)}), bf16[8704,256]{1,0:T(8,128)(2,1)}) %all-gather.5.cloned.1.call-update) | async-done | bytes 4456464 | tf_op jit(solution)/shard_map/all_gather | solution.py:21
  119.9 2.8 select_reduce_fusion
  122.7 0.9 fusion.5
  123.6 0.8 fusion.22
  124.5 15.0 %all_to_all.30 = bf16[16,8,512]{2,0,1:T(8,128)(2,1)S(1)} all-to-all(bf16[16,8,512]{2,0,1:T(8,128)(2,1)S(1)} %concatenate.19), channel_id=1, replica_groups=mesh['groups'=2,'seq_0'=16,'seq_1'=2,'rep'=8] {'rep'}, dimensions={1} | all-to-all | bytes 262144 | tf_op jit(solution)/shard_map/all_to_all | solution.py:16
  139.6 54.4 %all-gather.7.cloned.1.call-done = bf16[4096,512]{1,0:T(8,128)(2,1)} async-done(((bf16[128,512]{1,0:T(8,128)(2,1)}), bf16[4096,512]{1,0:T(8,128)(2,1)}) %all-gather.7.cloned.1.call-update) | async-done | bytes 4194320 | tf_op jit(solution)/shard_map/all_gather | solution.py:129
  194.0 2.9 fusion.16
  196.9 0.7 broadcast_in_dim.33
  197.5 7.2 %all-to-all-start.1 = ((bf16[8,16,512]{2,1,0:T(8,128)(2,1)}), bf16[8,16,512]{2,1,0:T(8,128)(2,1)S(1)}, u32[]{:S(2)}, u32[]{:S(2)}) async-start(bf16[8,16,512]{2,1,0:T(8,128)(2,1)} %broadcast_in_dim.33), calls=%async_computation.1 | async-start | bytes 262144 | tf_op jit(solution)/shard_map/all_to_all | solution.py:30
  204.8 8.0 %all-to-all-done.1 = bf16[8,16,512]{2,1,0:T(8,128)(2,1)S(1)} async-done(((bf16[8,16,512]{2,1,0:T(8,128)(2,1)}), bf16[8,16,512]{2,1,0:T(8,128)(2,1)S(1)}, u32[]{:S(2)}, u32[]{:S(2)}) %all-to-all-start.1) | async-done | bytes 131104 | tf_op jit(solution)/shard_map/all_to_all | solution.py:30
  213.7 0.9 fusion.1
  214.7 68.2 %all-gather.9.cloned.1.call-done = bf16[32,12,4096]{2,1,0:T(8,128)(2,1)} async-done(((bf16[1,12,4096]{2,1,0:T(8,128)(2,1)}), bf16[32,12,4096]{2,1,0:T(8,128)(2,1)}) %all-gather.9.cloned.1.call-update) | async-done | bytes 3145744 | tf_op jit(solution)/shard_map/all_gather | solution.py:159
  283.0 5.6 %reshape.183 = bf16[384,4096]{1,0:T(8,128)(2,1)} reshape(bf16[32,12,4096]{2,1,0:T(8,128)(2,1)} %all-gather.9.cloned.1.call-done) | data formatting | bytes 6291456
  288.6 2.9 fusion.30
  291.6 7.0 %convolution_convert_fusion = bf16[384,4096]{1,0:T(8,128)(2,1)} fusion(bf16[384,4096]{1,0:T(8,128)(2,1)} %reshape.183, bf16[1,128,4096]{2,1,0:T(8,128)(2,1)S(1)} %copy-done, bf16[1,4096,128]{2,1,0:T(8,128)(2,1)S(1)} %copy-done.2, f32[384,128]{1,0:T(8,128)S(1)} %fusion.30), kind=kOutput, calls=%fused_computation.2 | convolution fusion | flops 807174144 | bytes 8585216 | tf_op jit(solution)/shard_map/dot_general | solution.py:164
  298.6 5.5 %reshape_reshape.3 = bf16[16,2,12,4096]{3,2,1,0:T(8,128)(2,1)} reshape(bf16[384,4096]{1,0:T(8,128)(2,1)} %convolution_convert_fusion) | data formatting | bytes 6291456 | tf_op jit(solution)/shard_map/reshape;reshape | solution.py:48
  304.1 5.6 %copy.63 = bf16[2,16,12,4096]{3,1,0,2:T(8,128)(2,1)} copy(bf16[2,16,12,4096]{3,2,0,1:T(8,128)(2,1)} %bitcast.64) | data formatting | bytes 6291456 | tf_op jit(solution)/shard_map/transpose | solution.py:49
  309.8 19.7 %reduce-scatter.3.cloned.1.call-done = bf16[16,12,4096]{2,0,1:T(8,128)(2,1)} async-done(((bf16[32,12,4096]{2,0,1:T(8,128)(2,1)}), bf16[16,12,4096]{2,0,1:T(8,128)(2,1)}) %reduce-scatter.3.cloned.1.call-update) | async-done | bytes 1572880 | tf_op jit(solution)/shard_map/reduce_scatter | solution.py:52
  329.5 3.7 copy.64
  333.3 22.4 %all_gather.15 = bf16[32,1024]{1,0:T(8,128)(2,1)S(1)} all-gather(bf16[32,128]{1,0:T(8,128)(2,1)S(1)} %pad_maximum_fusion), channel_id=1, replica_groups=mesh['groups'=2,'seq_0'=16,'seq_1'=2,'rep'=8] {'rep'}, dimensions={1}, use_global_device_ids=true | all-gather | bytes 73728 | tf_op jit(solution)/shard_map/all_gather | solution.py:21
  355.6 0.6 fusion.72
  356.3 55.0 %reduce-scatter.5.cloned.1.call-done = bf16[1,12,4096]{2,1,0:T(8,128)(2,1)} async-done(((bf16[16,12,4096]{2,1,0:T(8,128)(2,1)}), bf16[1,12,4096]{2,1,0:T(8,128)(2,1)}) %reduce-scatter.5.cloned.1.call-update) | async-done | bytes 98320 | tf_op jit(solution)/shard_map/reduce_scatter | solution.py:52
  411.2 0.9 copy.70
  412.2 0.7 copy.65
  412.9 7.3 %all-to-all-start.2 = ((bf16[12,8,512]{2,0,1:T(8,128)(2,1)}), bf16[12,8,512]{2,0,1:T(8,128)(2,1)S(1)}, u32[]{:S(2)}, u32[]{:S(2)}) async-start(bf16[12,8,512]{2,0,1:T(8,128)(2,1)} %copy.65), calls=%async_computation.4 | async-start | bytes 262144 | tf_op jit(solution)/shard_map/all_to_all | solution.py:169
  420.4 7.4 %all-to-all-done.2 = bf16[12,8,512]{2,0,1:T(8,128)(2,1)S(1)} async-done(((bf16[12,8,512]{2,0,1:T(8,128)(2,1)}), bf16[12,8,512]{2,0,1:T(8,128)(2,1)S(1)}, u32[]{:S(2)}, u32[]{:S(2)}) %all-to-all-start.2) | async-done | bytes 98336 | tf_op jit(solution)/shard_map/all_to_all | solution.py:169
  427.8 0.8 fusion.15
  (56 shorter events, 1.7 us)
Async XLA Ops:
  7.2 284.4 %copy-start = (bf16[1,128,4096]{2,1,0:T(8,128)(2,1)S(1)}, bf16[1,128,4096]{2,1,0:T(8,128)(2,1)}, u32[]{:S(2)}) copy-start(bf16[1,128,4096]{2,1,0:T(8,128)(2,1)} %param.26) | copy-start | bytes 3145732
  7.2 112.7 %all-gather.5.cloned.1.call-start = ((), (), s32[]{:S(2)}) async-start(), calls=%async_computation.5 | async-start | bytes 4595712 | tf_op jit(solution)/shard_map/all_gather | solution.py:21
  9.0 185.0 %all-gather.7.cloned.1.call-start = ((), (), s32[]{:S(2)}) async-start(), calls=%async_computation.6 | async-start | bytes 4325376 | tf_op jit(solution)/shard_map/all_gather | solution.py:129
  119.9 3.7 copy-start.10
  123.6 70.4 %copy-start.6 = (bf16[16,512]{1,0:T(8,128)(2,1)S(1)}, bf16[16,512]{1,0:T(8,128)(2,1)}, u32[]{:S(2)}) copy-start(bf16[16,512]{1,0:T(8,128)(2,1)} %param.20) | copy-start | bytes 49156
  194.0 10.8 %copy-start.9 = (s32[16,2]{0,1:T(2,128)S(1)}, s32[16,2]{0,1:T(2,128)}, u32[]{:S(2)}) copy-start(s32[16,2]{0,1:T(2,128)} %param.27) | copy-start | bytes 388
  194.0 19.0 %copy-start.4 = (f32[4096,4]{0,1:T(4,128)S(1)}, f32[4096,4]{0,1:T(4,128)}, u32[]{:S(2)}) copy-start(f32[4096,4]{0,1:T(4,128)} %param.23) | copy-start | bytes 196612
  194.0 19.0 %copy-start.5 = (f32[4096]{0:T(1024)S(1)}, f32[4096]{0:T(1024)}, u32[]{:S(2)}) copy-start(f32[4096]{0:T(1024)} %param.22) | copy-start | bytes 49156
  196.9 230.9 %copy-start.3 = (bf16[16,512]{1,0:T(8,128)(2,1)}, bf16[16,512]{1,0:T(8,128)(2,1)S(1)}, u32[]{:S(2)}) copy-start(bf16[16,512]{1,0:T(8,128)(2,1)S(1)} %fusion.16) | copy-start | bytes 49156
  197.5 15.2 %all-to-all-start.1 = ((bf16[8,16,512]{2,1,0:T(8,128)(2,1)}), bf16[8,16,512]{2,1,0:T(8,128)(2,1)S(1)}, u32[]{:S(2)}, u32[]{:S(2)}) async-start(bf16[8,16,512]{2,1,0:T(8,128)(2,1)} %broadcast_in_dim.33), calls=%async_computation.1 | async-start | bytes 262144 | tf_op jit(solution)/shard_map/all_to_all | solution.py:30
  204.8 78.2 %all-gather.9.cloned.1.call-start = ((), (), s32[]{:S(2)}) async-start(), calls=%async_computation.9 | async-start | bytes 4325376 | tf_op jit(solution)/shard_map/all_gather | solution.py:159
  214.7 73.9 %copy-start.1 = (bf16[1,4096,128]{2,1,0:T(8,128)(2,1)S(1)}, bf16[1,4096,128]{2,1,0:T(8,128)(2,1)}, u32[]{:S(2)}) copy-start(bf16[1,4096,128]{2,1,0:T(8,128)(2,1)} %param.24) | copy-start | bytes 3145732
  214.7 114.8 %reduce-scatter.3.cloned.1.call-start = ((), (), s32[]{:S(2)}) async-start(), calls=%async_computation.7 | async-start | bytes 4718592 | tf_op jit(solution)/shard_map/reduce_scatter | solution.py:52
  288.6 3.0 copy-start.2
  309.7 23.5 %copy-start.7 = (bf16[16,128]{1,0:T(8,128)(2,1)S(1)}, bf16[16,128]{1,0:T(8,128)(2,1)}, u32[]{:S(2)}) copy-start(bf16[16,128]{1,0:T(8,128)(2,1)} %param.16) | copy-start | bytes 12292
  309.7 23.5 %copy-start.8 = (bf16[16,128]{1,0:T(8,128)(2,1)S(1)}, bf16[16,128]{1,0:T(8,128)(2,1)}, u32[]{:S(2)}) copy-start(bf16[16,128]{1,0:T(8,128)(2,1)} %param.15) | copy-start | bytes 12292
  309.7 101.5 %reduce-scatter.5.cloned.1.call-start = ((), (), s32[]{:S(2)}) async-start(), calls=%async_computation.8 | async-start | bytes 2228224 | tf_op jit(solution)/shard_map/reduce_scatter | solution.py:52
  412.9 14.9 %all-to-all-start.2 = ((bf16[12,8,512]{2,0,1:T(8,128)(2,1)}), bf16[12,8,512]{2,0,1:T(8,128)(2,1)S(1)}, u32[]{:S(2)}, u32[]{:S(2)}) async-start(bf16[12,8,512]{2,0,1:T(8,128)(2,1)} %copy.65), calls=%async_computation.4 | async-start | bytes 262144 | tf_op jit(solution)/shard_map/all_to_all | solution.py:169
Sparse Core Ops, SparseCore 0:
  10.2 109.7 all-gather.4
  122.1 71.8 all-gather.6
  214.8 68.1 all-gather.8
  309.8 19.6 reduce-scatter.2
  333.4 77.8 reduce-scatter.4
